TPU v7x, 32 devices: a whole 2x2x4 slice. The times are simulated.
32 devices in a mesh: groups: 2 (over y), seq: 4 (over z), section: 2 (over x), tp: 2 (over core).
Axes of the slice: x: 2, y: 2, z: 4, core: 2. Of those that a mesh axis runs over, the one named last changes fastest.
Arguments:
- qkv: bfloat16 [4, 1024, 3, 2048], P(('groups', 'section'), ('seq', 'tp')), parts along dimension 0, may hold values from -100 to 100
- stream: bfloat16 [4, 1024, 3072], P(('groups', 'section'), ('seq', 'tp')), parts along dimension 0, may hold values from -6 to 6
- out_weight: bfloat16 [2048, 3072], P('tp'), may hold values from -0.125 to 0.125
- mod_scale: float32 [4, 3072], P(('groups', 'section')), parts along dimension 0, may hold values from -3 to 3
- mod_shift: float32 [4, 3072], P(('groups', 'section')), parts along dimension 0, may hold values from -3 to 3
- final_weight: bfloat16 [3072, 64], replicated, may hold values from -0.109375 to 0.109375
- latent: float32 [4, 1024, 64], P(('groups', 'section'), ('seq', 'tp')), parts along dimension 0, may hold values from -6 to 6
- step_size: float32 [4], P(('groups', 'section')), parts along dimension 0, may hold values from 0.2 to 1
- frame_counts: int32 [4, 4], P(('groups', 'section')), parts along dimension 0, may hold values from 1 to 4, 8 in all within a row
- finished: int32 [4, 4], P(('groups', 'section')), parts along dimension 0, may hold values 0 or 1
- conv_weight: bfloat16 [3, 3, 3, 16, 512], P(None, None, None, None, 'tp'), may hold values from -0.3125 to 0.3125
- conv_bias: float32 [512], P('tp'), may hold values from -3 to 3
- up_weight: bfloat16 [512, 512], P('tp'), may hold values from -0.25 to 0.25
- up_bias: float32 [512], P('tp'), may hold values from -3 to 3
Outputs:
- new_latent: float32 [4, 1024, 64], P(('groups', 'section'), ('seq', 'tp')), parts along dimension 0
- decoded: bfloat16 [4, 8, 16, 32, 512], P(('groups', 'section'), None, 'seq', None, 'tp'), parts along dimension 0
There are 2 independent parts, one for each index of `groups`. A program takes and returns all parts, laid end to end along the dimension named above; an argument that names none is the same for every part. Nothing has to cross between parts.
Inputs may be any that keep to these rules, and one draw needn't show every extreme that they name: `frame_counts`: a part's 4 requests are packed in order and their frame counts sum to 8.
All inputs are finite; a program needn't handle non-finite values. No bound on the sum of `finished` on one device may be relied on, other than what follows from the above.
Results may differ from a plain program's by a relative error of at most 0.012.
Values may be sent and summed in bfloat16 or wider, within the bound.
A program may use at most 64 MiB of HBM per device.

v0:
```python
import math

import jax
import jax.numpy as jnp
from jax import lax
from jax.experimental import pallas as pl
from jax.experimental.pallas import tpu as pltpu
from jax.sharding import PartitionSpec as P

HEADS = 16
HD = 128
LATC = 16
PROWS = 8
PCOLS = 16
F_TOK = 128
LROWS = 16
LCOLS = 32


EPSILON = 1e-06
NEG_FILL = -1e30


def padded_2(value, sides, width):
    for axis, dim in sides:
        peers, length = (lax.axis_size(axis), value.shape[dim])
        up = [(i, (i + 1) % peers) for i in range(peers - 1)]
        down = [(j, i) for i, j in up]
        last = lax.slice_in_dim(value, length - width, length, axis=dim)
        initial = lax.slice_in_dim(value, 0, width, axis=dim)
        before = lax.ppermute(last, axis, up)
        after = lax.ppermute(initial, axis, down)
        value = jnp.concatenate([before, value, after], axis=dim)
    return value


def request_index(positions, counts, unit):
    ends = jnp.cumsum(counts) * unit
    return jnp.sum((positions[:, None] >= ends[None, :]).astype(jnp.int32), axis=1)


def attend_block(running, queries, query_req, key_rows, value_rows, key_req):
    running_max, weight_sum, accumulated = running
    scores = jnp.einsum("qhd,khd->qhk", queries, key_rows, preferred_element_type=jnp.float32) * (
        1.0 / math.sqrt(queries.shape[2])
    )
    allowed = (query_req[:, None] == key_req[None, :])[:, None, :]
    masked = jnp.where(allowed, scores, NEG_FILL)
    new_max = jnp.maximum(running_max, jnp.max(masked, axis=2))
    weights = jnp.where(allowed, jnp.exp(masked - new_max[:, :, None]), 0.0)
    factor = jnp.exp(running_max - new_max)
    weight_sum = weight_sum * factor + jnp.sum(weights, axis=2)
    product = jnp.einsum(
        "qhk,khd->qhd", weights.astype(jnp.bfloat16), value_rows, preferred_element_type=jnp.float32
    )
    accumulated = accumulated * factor[:, :, None] + product
    return (new_max, weight_sum, accumulated)


def fold_keys(running, queries, query_req, key_rows, value_rows, key_req):
    row_count = key_rows.shape[0]
    lowest = jnp.min(query_req)
    highest = jnp.max(query_req)

    def key_block(folded, block_data):
        block_keys, block_values, block_req = block_data
        touches = jnp.logical_and(jnp.min(block_req) <= highest, jnp.max(block_req) >= lowest)
        result = lax.cond(
            touches,
            lambda current: attend_block(
                current, queries, query_req, block_keys, block_values, block_req
            ),
            lambda current: current,
            folded,
        )
        return (result, None)

    pieces = row_count // 512
    shaped_keys = key_rows.reshape(pieces, 512, key_rows.shape[1], key_rows.shape[2])
    shaped_values = value_rows.reshape(pieces, 512, value_rows.shape[1], value_rows.shape[2])
    shaped_req = key_req.reshape(pieces, 512)
    folded, _ = lax.scan(key_block, running, (shaped_keys, shaped_values, shaped_req))
    return folded


def empty_state(queries):
    query_rows, heads_here, head_size = queries.shape
    return (
        jnp.full((query_rows, heads_here), NEG_FILL, jnp.float32),
        jnp.zeros((query_rows, heads_here), jnp.float32),
        jnp.zeros((query_rows, heads_here, head_size), jnp.float32),
    )


def normalize(folded):
    return (folded[2] / folded[1][:, :, None]).astype(jnp.bfloat16)


def on_device(
    qkv,
    stream,
    out_weight,
    mod_scale,
    mod_shift,
    final_weight,
    latent,
    step_size,
    frame_counts,
    finished,
    conv_weight,
    conv_bias,
    up_weight,
    up_bias,
):
    tp_count = lax.axis_size("tp")
    tp_place = lax.axis_index("tp")
    token_rows = qkv.shape[1]
    counts = frame_counts[0]
    done_flags = finished[0]
    packed = qkv[0].reshape(token_rows, 3, HEADS, HD)
    regrouped = lax.all_to_all(packed, "seq", split_axis=2, concat_axis=0, tiled=True)
    local_rows = regrouped.shape[0]
    positions = jnp.arange(local_rows, dtype=jnp.int32)
    token_queries = (
        positions // token_rows * tp_count + tp_place
    ) * token_rows + positions % token_rows
    query_req = request_index(token_queries // F_TOK, counts, 1)
    queries = regrouped[:, 0]
    key_portion = (
        lax.all_gather(regrouped[:, 1], "tp", axis=0, tiled=True),
        lax.all_gather(regrouped[:, 2], "tp", axis=0, tiled=True),
    )
    key_index = jnp.arange(key_portion[0].shape[0], dtype=jnp.int32)
    source = key_index // local_rows
    within = key_index % local_rows
    key_tokens = (within // token_rows * tp_count + source) * token_rows + within % token_rows
    folded = fold_keys(
        empty_state(queries),
        queries,
        query_req,
        key_portion[0],
        key_portion[1],
        request_index(key_tokens // F_TOK, counts, 1),
    )
    returned = lax.all_to_all(
        lax.all_to_all(normalize(folded), "seq", split_axis=0, concat_axis=1, tiled=True),
        "tp",
        split_axis=1,
        concat_axis=0,
        tiled=True,
    )
    flattened = returned.reshape(returned.shape[0], returned.shape[1] * returned.shape[2])
    summed = lax.psum_scatter(
        jnp.dot(flattened, out_weight, preferred_element_type=jnp.float32).astype(jnp.bfloat16),
        "tp",
        scatter_dimension=0,
        tiled=True,
    ).astype(jnp.float32)
    mixed_stream = stream[0].astype(jnp.float32) + summed
    average = jnp.mean(mixed_stream, axis=1, keepdims=True)
    centred = mixed_stream - average
    variance = jnp.mean(centred * centred, axis=1, keepdims=True)
    normed = centred / jnp.sqrt(variance + EPSILON)
    modulated = (normed * (1.0 + mod_scale[0]) + mod_shift[0]).astype(jnp.bfloat16)
    velocity = jnp.dot(modulated, final_weight, preferred_element_type=jnp.float32)
    updated = latent[0] + step_size[0] * velocity
    frame_local = token_rows // F_TOK
    own_video = updated.reshape(frame_local, PROWS, PCOLS, 2, 2, LATC).transpose(0, 1, 3, 2, 4, 5)
    own_video = own_video.reshape(frame_local, LROWS, LCOLS, LATC).astype(jnp.bfloat16)
    matched_pairs = lax.all_gather(own_video, "tp", axis=0, tiled=True)
    slab_grouped = lax.all_to_all(matched_pairs, "seq", split_axis=1, concat_axis=0, tiled=True)
    frame_count_total = slab_grouped.shape[0]
    rows_per_slab = slab_grouped.shape[1]
    with_halo_rows = padded_2(slab_grouped, (("seq", 1),), 1)
    padded = jnp.pad(with_halo_rows, ((2, 0), (0, 0), (1, 1), (0, 0)))
    frame_ids = jnp.arange(frame_count_total, dtype=jnp.int32)
    owner_req = request_index(frame_ids, counts, 1)
    starts = jnp.cumsum(counts) - counts
    selector = owner_req[:, None] == jnp.arange(counts.shape[0], dtype=jnp.int32)[None, :]
    first_frame = jnp.sum(jnp.where(selector, starts[None, :], 0), axis=1)
    alive_frame = jnp.sum(jnp.where(selector, done_flags[None, :], 0), axis=1)
    columns_list = []
    for time_tap in range(3):
        inside = frame_ids - 2 + time_tap >= first_frame
        for row_tap in range(3):
            for col_tap in range(3):
                window = padded[
                    time_tap : time_tap + frame_count_total,
                    row_tap : row_tap + rows_per_slab,
                    col_tap : col_tap + LCOLS,
                ]
                columns_list.append(
                    jnp.where(inside[:, None, None, None], window, jnp.zeros_like(window))
                )
    stacked = jnp.concatenate(columns_list, axis=3).reshape(-1, 27 * LATC)
    whole_kernel, whole_bias = (
        lax.all_gather(
            conv_weight.astype(jnp.float32).astype(jnp.bfloat16), "tp", axis=4, tiled=True
        ).astype(jnp.float32),
        lax.all_gather(conv_bias.astype(jnp.bfloat16), "tp", axis=0, tiled=True).astype(
            conv_bias.dtype
        ),
    )
    kernel = whole_kernel.astype(jnp.bfloat16).reshape(27 * LATC, whole_kernel.shape[4])
    hidden = jax.nn.silu(
        jnp.dot(stacked, kernel, preferred_element_type=jnp.float32) + whole_bias
    ).astype(jnp.bfloat16)
    own_columns = lax.all_to_all(up_weight, "tp", split_axis=1, concat_axis=0, tiled=True)
    shared = jnp.dot(hidden, own_columns, preferred_element_type=jnp.float32).reshape(
        frame_count_total, rows_per_slab, LCOLS, own_columns.shape[1]
    )
    decoded = ((shared + up_bias) * alive_frame.astype(jnp.float32)[:, None, None, None]).astype(
        jnp.bfloat16
    )
    return (updated[None], decoded[None])


NN = (((1,), (0,)), ((), ()))
NT = (((1,), (1,)), ((), ()))


def request_of(frame, ends):
    owner = (frame >= ends[0]).astype(jnp.int32)
    for end in ends[1:]:
        owner = owner + (frame >= end).astype(jnp.int32)
    return owner


def frame_ends(counts_ref, requests):
    ends = [counts_ref[0, 0]]
    for i in range(1, requests):
        ends.append(ends[-1] + counts_ref[0, i])
    return ends


def slab_start(seq, rows):
    return jnp.clip(seq * rows - 1, 0, PROWS - rows - 2)


def expand_weight(kernel_ref, expanded_ref, patch):
    for i in range(2):
        for j in range(2):
            for a in range(3):
                for dr in range(2):
                    for dc in range(2):
                        for i2 in range(2):
                            for j2 in range(2):
                                b = i - 1 + 2 * dr + i2
                                e = j - 1 + 2 * dc + j2
                                if 0 <= b < 3 and 0 <= e < 3:
                                    to = ((a * 2 + dr) * 2 + dc) * patch + (i2 * 2 + j2) * LATC
                                    come = ((a * 3 + b) * 3 + e) * LATC
                                    expanded_ref[i * 2 + j, to : to + LATC] = kernel_ref[come : come + LATC]


def attend_kernel(
    n,
    window,
    requests,
    qkv_ref,
    stream_ref,
    ow_ref,
    scale_hbm,
    shift_hbm,
    fw_hbm,
    latent_hbm,
    step_hbm,
    counts_ref,
    finished_ref,
    cw_ref,
    cb_ref,
    uw_ref,
    ub_hbm,
    new_latent_ref,
    decoded_ref,
    video_ref,
    expanded_ref,
    cb2_ref,
    uw2_ref,
    ub_ref,
    shifted,
    columns,
    spread,
    qkv_buf,
    cw2_ref,
    scale_ref,
    shift_ref,
    fw_ref,
    latent_ref,
    step_ref,
    q_buf,
    kv_buf,
    w_buf,
    stream_buf,
    bias_buf,
    max_buf,
    sum_buf,
    acc_buf,
    att_buf,
    part_buf,
    got_buf,
    mixed_buf,
    own_video,
    local_sems,
    q_sems,
    kv_send,
    kv_recv,
    part_send,
    part_recv,
    wt_send,
    wt_recv,
    vid_send,
    vid_recv,
):
    s = lax.axis_index("seq")
    t = lax.axis_index("tp")
    o = 1 - t
    me = s * 2 + t
    devices = 2 * n
    half = q_buf.shape[2]
    heads = half // HD
    hops = (window + 1) // 2
    out_half = uw_ref.shape[1] // 2
    ccols = cw_ref.shape[1]

    def at(seq, tp):
        return {"seq": seq, "tp": tp}

    def remote(src, dst, send, recv, target):
        return pltpu.make_async_remote_copy(
            src_ref=src,
            dst_ref=dst,
            send_sem=send,
            recv_sem=recv,
            device_id=target,
            device_id_type=pl.DeviceIdType.MESH,
        )

    def peer_of(k):
        peer = lax.rem(me + k, devices)
        return at(peer // 2, lax.rem(peer, 2))

    def cols(which, width):
        return pl.ds(pl.multiple_of(which * width, width), width)

    own_q = pltpu.make_async_copy(qkv_ref.at[0, :, cols(t, half)], q_buf.at[1], local_sems.at[0])
    own_kv = pltpu.make_async_copy(
        qkv_ref.at[1:3, :, cols(t, half)], kv_buf.at[window + t], local_sems.at[1]
    )
    get_w = pltpu.make_async_copy(ow_ref, w_buf, local_sems.at[2])
    get_stream = pltpu.make_async_copy(stream_ref, stream_buf, local_sems.at[3])
    stage = pltpu.make_async_copy(qkv_ref, qkv_buf, local_sems.at[13])
    stage.start()
    own_q.start()
    own_kv.start()

    barrier = pltpu.get_barrier_semaphore()
    for k in range(1, devices):
        pl.semaphore_signal(
            barrier, inc=1, device_id=peer_of(k), device_id_type=pl.DeviceIdType.MESH
        )
    pl.semaphore_wait(barrier, devices - 1)
    stage.wait()

    def kv_copy(target_tp, target_seq, slot, send):
        return remote(
            qkv_buf.at[1:3, :, cols(target_tp, half)],
            kv_buf.at[slot],
            kv_send.at[send],
            kv_recv.at[slot],
            at(target_seq, target_tp),
        )

    has_left = s > 0
    has_right = s < n - 1
    rights = [kv_copy(k, s + 1, window + t - 2, k) for k in range(2)]
    lefts = [kv_copy(k, s - 1, window + t + 2, 2 + k) for k in range(2)]
    partner_q = remote(
        qkv_buf.at[0, :, cols(o, half)], q_buf.at[0], q_sems.at[0], q_sems.at[1], at(s, o)
    )
    partner_kv = kv_copy(o, s, window + t, 4)

    @pl.when(has_right)
    def _():
        for copy in rights:
            copy.start()

    @pl.when(has_left)
    def _():
        for copy in lefts:
            copy.start()

    partner_q.start()
    partner_kv.start()
    give_cw = remote(cw_ref, cw2_ref.at[:, ccols:], wt_send.at[0], wt_recv.at[0], at(s, o))
    give_cb = remote(cb_ref, cb2_ref.at[:, ccols:], wt_send.at[1], wt_recv.at[1], at(s, o))
    give_uw = remote(
        uw_ref.at[:, cols(o, out_half)],
        uw2_ref.at[pl.ds(uw_ref.shape[0], uw_ref.shape[0])],
        wt_send.at[2],
        wt_recv.at[2],
        at(s, o),
    )
    give_cw.start()
    give_cb.start()
    give_uw.start()
    loads = [
        pltpu.make_async_copy(source, target, local_sems.at[4 + i])
        for i, (source, target) in enumerate(
            (
                (cw_ref, cw2_ref.at[:, :ccols]),
                (cb_ref, cb2_ref.at[:, :ccols]),
                (uw_ref.at[:, cols(t, out_half)], uw2_ref.at[: uw_ref.shape[0]]),
                (scale_hbm, scale_ref),
                (shift_hbm, shift_ref),
                (fw_hbm, fw_ref),
                (latent_hbm, latent_ref),
                (step_hbm, step_ref),
                (ub_hbm, ub_ref),
            )
        )
    ]
    for load in loads:
        load.start()
    get_stream.start()
    get_w.start()

    ends = frame_ends(counts_ref, requests)
    query_req = (request_of(s * 2 + o, ends), request_of(s * 2 + t, ends))
    score_scale = 1.0 / math.sqrt(HD)

    def wait_slot(slot):
        remote(kv_buf.at[slot], kv_buf.at[slot], kv_send.at[0], kv_recv.at[slot], at(s, o)).wait_recv()

    def attend_far(slot, place, query_frame):
        key_req = request_of(s * 2 - window + slot, ends)
        bias = jnp.where(request_of(query_frame, ends) == key_req, 0.0, NEG_FILL).astype(jnp.float32)
        rows = pl.ds(pl.multiple_of(place * F_TOK, F_TOK), F_TOK)

        def one_head(h, carry):
            lanes = pl.ds(pl.multiple_of(h * HD, HD), HD)
            q = q_buf[place, :, lanes]
            scores = lax.dot_general(
                q, kv_buf[slot, 0, :, lanes], NT, preferred_element_type=jnp.float32
            )
            scores = scores * score_scale + bias
            old = max_buf[h, rows, :]
            top = jnp.maximum(old, jnp.max(scores, axis=1, keepdims=True))
            weights = jnp.exp(scores - top)
            factor = jnp.exp(old - top)
            sum_buf[h, rows, :] = sum_buf[h, rows, :] * factor + jnp.sum(
                weights, axis=1, keepdims=True
            )
            acc_buf[h, rows, :] = acc_buf[h, rows, :] * factor + lax.dot_general(
                weights.astype(jnp.bfloat16),
                kv_buf[slot, 1, :, lanes],
                NN,
                preferred_element_type=jnp.float32,
            )
            return carry

        lax.fori_loop(0, heads, one_head, 0, unroll=True)

    def attend(first, width, fresh):
        for i in range(2):
            for j in range(width):
                key_req = request_of(s * 2 - window + first + j, ends)
                bias = jnp.where(query_req[i] == key_req, 0.0, NEG_FILL).astype(jnp.float32)
                bias_buf[pl.ds(i * F_TOK, F_TOK), pl.ds(j * F_TOK, F_TOK)] = jnp.full(
                    (F_TOK, F_TOK), bias, jnp.float32
                )
        bias = bias_buf[:, : width * F_TOK]

        def one_head(h, carry):
            lanes = pl.ds(pl.multiple_of(h * HD, HD), HD)
            q = q_buf[:, :, lanes].reshape(2 * F_TOK, HD)
            keys = kv_buf[first : first + width, 0, :, lanes].reshape(width * F_TOK, HD)
            values = kv_buf[first : first + width, 1, :, lanes].reshape(width * F_TOK, HD)
            scores = lax.dot_general(q, keys, NT, preferred_element_type=jnp.float32)
            scores = scores * score_scale + bias
            top = jnp.max(scores, axis=1, keepdims=True)
            if not fresh:
                old = max_buf[h]
                top = jnp.maximum(old[:, :1], top)
            weights = jnp.exp(scores - top)
            total = jnp.sum(weights, axis=1, keepdims=True)
            product = lax.dot_general(
                weights.astype(jnp.bfloat16), values, NN, preferred_element_type=jnp.float32
            )
            if not fresh:
                factor = jnp.exp(old[:, :1] - top)
                total = total + sum_buf[h][:, :1] * factor
                product = product + acc_buf[h] * factor
            max_buf[h] = jnp.broadcast_to(top, (2 * F_TOK, HD))
            sum_buf[h] = jnp.broadcast_to(total, (2 * F_TOK, HD))
            acc_buf[h] = product
            return carry

        lax.fori_loop(0, heads, one_head, 0, unroll=4)

    own_q.wait()
    own_kv.wait()
    partner_q.wait_recv()
    wait_slot(window + o)
    attend(window, 2, True)

    loads[0].wait()
    give_cw.wait()
    expanded_ref[...] = jnp.zeros_like(expanded_ref)
    expand_weight(cw2_ref, expanded_ref, new_latent_ref.shape[0])

    relays = []
    for d in range(1, hops + 1):
        low = window - 2 * d
        high = window + 2 * d
        two = 2 * d <= window
        more = d < hops

        def receive(first, width, good, forward, good_next, step, base, sends):
            @pl.when(good)
            def _():
                for j in range(width):
                    wait_slot(first + j)

            copies = []
            if forward:
                for slot in forward:
                    copies.append(
                        remote(
                            kv_buf.at[slot],
                            kv_buf.at[slot - 2 * step],
                            kv_send.at[sends + len(copies)],
                            kv_recv.at[slot - 2 * step],
                            at(s + step, t),
                        )
                    )

                @pl.when(good_next)
                def _():
                    for copy in copies:
                        copy.start()

            return [(copy, good_next) for copy in copies]

        base = 5 + 4 * (d - 1)
        wide = 2 if two else 1
        next_two = 2 * (d + 1) <= window
        left_first = low if two else low + 1
        left_good = s >= d
        right_good = s <= n - 1 - d
        left_fwd = ([low, low + 1] if next_two else [low + 1]) if more else []
        right_fwd = ([high, high + 1] if next_two else [high]) if more else []
        def attend_left():
            @pl.when(left_good)
            def _():
                if two:
                    attend(left_first, 2, False)
                else:
                    attend_far(left_first, o, s * 2)

        relays += receive(
            left_first, wide, left_good, left_fwd, jnp.logical_and(left_good, has_right), 1, d, base
        )
        if not more:
            attend_left()
        relays += receive(
            high, wide, right_good, right_fwd, jnp.logical_and(right_good, has_left), -1, d, base + 2
        )
        if more:
            attend_left()

        @pl.when(right_good)
        def _():
            if two:
                attend(high, 2, False)
            else:
                attend_far(high, t, s * 2 + 1)

    for h in range(heads):
        att_buf[:, h * HD : (h + 1) * HD] = (acc_buf[h] / sum_buf[h]).astype(jnp.bfloat16)

    get_w.wait()
    get_stream.wait()
    for load in loads[1:]:
        load.wait()
    chunks, _, chunk = part_buf.shape
    attended = att_buf[...]
    parts = []
    for c in range(chunks):
        span = pl.ds(c * chunk, chunk)
        result = lax.dot_general(attended, w_buf[:, span], NN, preferred_element_type=jnp.float32)
        part_buf[c] = result[:F_TOK].astype(jnp.bfloat16)
        copy = remote(part_buf.at[c], got_buf.at[c], part_send.at[c], part_recv.at[c], at(s, o))
        copy.start()
        parts.append(copy)
        mixed_buf[:, span] = result[F_TOK:] + stream_buf[:, span].astype(jnp.float32)
    row_sum = jnp.zeros((F_TOK, 1), jnp.float32)
    for c in range(chunks):
        span = pl.ds(c * chunk, chunk)
        parts[c].wait_recv()
        mixed = mixed_buf[:, span] + got_buf[c].astype(jnp.float32)
        mixed_buf[:, span] = mixed
        row_sum = row_sum + jnp.sum(mixed, axis=1, keepdims=True)
    width = mixed_buf.shape[1]
    average = row_sum / width
    row_square = jnp.zeros((F_TOK, 1), jnp.float32)
    for c in range(chunks):
        centred = mixed_buf[:, c * chunk : (c + 1) * chunk] - average
        row_square = row_square + jnp.sum(centred * centred, axis=1, keepdims=True)
    inverse = 1.0 / jnp.sqrt(row_square / width + EPSILON)
    velocity = jnp.zeros((fw_ref.shape[0], F_TOK), jnp.float32)
    for c in range(chunks):
        span = pl.ds(c * chunk, chunk)
        normed = (mixed_buf[:, span] - average) * inverse
        modulated = (normed * (1.0 + scale_ref[:, span]) + shift_ref[:, span]).astype(jnp.bfloat16)
        velocity = velocity + lax.dot_general(
            fw_ref[:, span], modulated, NT, preferred_element_type=jnp.float32
        )
    updated = latent_ref[...] + step_ref[0] * velocity
    new_latent_ref[...] = updated
    own_video[...] = updated.T.astype(jnp.bfloat16)
    kept = video_ref.shape[1]

    def needed(seq):
        first = slab_start(seq, kept // PCOLS - 2) * PCOLS
        return pl.ds(pl.multiple_of(first, PCOLS), kept)

    sends = []
    for k in range(1, devices):
        target = peer_of(k)
        copy = remote(
            own_video.at[needed(target["seq"])],
            video_ref.at[me],
            vid_send.at[k - 1],
            vid_recv.at[k - 1],
            target,
        )
        copy.start()
        sends.append(copy)
    video_ref[me] = own_video[needed(s), :]

    partner_q.wait_send()
    partner_kv.wait_send()

    @pl.when(has_right)
    def _():
        for copy in rights:
            copy.wait_send()

    @pl.when(has_left)
    def _():
        for copy in lefts:
            copy.wait_send()

    for copy, good in relays:

        @pl.when(good)
        def _(copy=copy):
            copy.wait_send()

    for copy in parts:
        copy.wait_send()
    give_cb.wait()
    give_uw.wait()
    for copy in sends:
        copy.wait()
    decode_frames(
        kept // PCOLS - 2,
        requests,
        video_ref,
        expanded_ref,
        cb2_ref,
        uw2_ref,
        ub_ref,
        counts_ref,
        finished_ref,
        decoded_ref,
        shifted,
        columns,
        spread,
    )


def decode_frames(
    rows,
    requests,
    video_ref,
    expanded,
    cb_ref,
    uw_ref,
    ub_ref,
    counts_ref,
    finished_ref,
    out_ref,
    shifted,
    columns,
    spread,
):
    s = lax.axis_index("seq")
    frames = video_ref.shape[0]
    group = rows + 2
    span = group * PCOLS
    patch = video_ref.shape[2]
    ends = frame_ends(counts_ref, requests)
    owners = [request_of(jnp.int32(f), ends) for f in range(frames)]

    pieces = []
    for f in range(frames):
        for r in range(group):
            row = s * rows + r - 1
            inside = jnp.logical_and(row >= 0, row < PROWS)
            clamped = jnp.clip(row, 0, PROWS - 1) - slab_start(s, rows)
            piece = video_ref[f, pl.ds(pl.multiple_of(clamped * PCOLS, PCOLS), PCOLS), :]
            pieces.append(jnp.where(inside, piece.astype(jnp.float32), 0.0))
    middle = jnp.concatenate(pieces, axis=0)
    total = frames * span
    column = lax.rem(lax.broadcasted_iota(jnp.int32, (total, patch), 0), PCOLS)
    before = jnp.where(column == 0, 0.0, pltpu.roll(middle, 1, 0))
    after = jnp.where(column == PCOLS - 1, 0.0, pltpu.roll(middle, total - 1, 0))
    shifted[0] = jnp.concatenate([before, middle], axis=1).astype(jnp.bfloat16)
    shifted[1] = jnp.concatenate([middle, after], axis=1).astype(jnp.bfloat16)

    block = rows * PCOLS
    lanes = 2 * patch
    for f in range(frames):
        for a in range(3):
            g = f - 2 + a
            for i in range(2):
                for dr in range(2):
                    for j in range(2):
                        place = pl.ds((a * 2 + dr) * lanes, lanes)
                        if g < 0:
                            value = jnp.zeros((block, lanes), jnp.bfloat16)
                        else:
                            first = g * span + (i + dr) * PCOLS
                            value = shifted[j, first : first + block]
                            if g != f:
                                keep = (owners[g] == owners[f]).astype(jnp.float32)
                                value = value * jnp.full((1, lanes), keep, jnp.float32).astype(
                                    jnp.bfloat16
                                )
                        columns[i * 2 + j, f * block : (f + 1) * block, place] = value

    alive = []
    for f in range(frames):
        flag = jnp.float32(0)
        for r in range(requests):
            flag = flag + jnp.where(owners[f] == r, finished_ref[0, r], 0).astype(jnp.float32)
        alive.append(flag)
    out_cols = uw_ref.shape[1]
    for i in range(2):
        for j in range(2):
            hidden = lax.dot_general(
                columns[i * 2 + j], expanded[i * 2 + j], NN, preferred_element_type=jnp.float32
            )
            hidden = jax.nn.silu(hidden + cb_ref[...]).astype(jnp.bfloat16)
            shared = lax.dot_general(hidden, uw_ref[...], NN, preferred_element_type=jnp.float32)
            shared = shared + ub_ref[...]
            for f in range(frames):
                for r in range(rows):
                    first = f * block + r * PCOLS
                    value = shared[first : first + PCOLS] * alive[f]
                    for c in range(out_cols // 128):
                        spread[c, f, 2 * r + i, pl.ds(j, PCOLS, stride=2), :] = value[
                            :, c * 128 : (c + 1) * 128
                        ]
    for c in range(out_cols // 128):
        out_ref[:, :, :, c * 128 : (c + 1) * 128] = spread[c].astype(jnp.bfloat16)


def on_device_fast(
    qkv,
    stream,
    out_weight,
    mod_scale,
    mod_shift,
    final_weight,
    latent,
    step_size,
    frame_counts,
    finished,
    conv_weight,
    conv_bias,
    up_weight,
    up_bias,
):
    n = lax.axis_size("seq")
    frames = 2 * n
    window = frames // 2 - 1
    requests = frame_counts.shape[1]
    width = stream.shape[2]
    patch = latent.shape[2]
    half = out_weight.shape[0]
    heads = half // HD
    ccols = conv_weight.shape[4]
    taps = conv_weight.shape[0] * conv_weight.shape[1] * conv_weight.shape[2] * LATC
    up_rows, up_all = up_weight.shape
    out_half = up_all // 2
    slots = 2 * window + 2
    hops = (window + 1) // 2
    rows = PROWS // n
    chunks = 6
    chunk = width // chunks
    vmem = pl.BlockSpec(memory_space=pltpu.VMEM)
    smem = pl.BlockSpec(memory_space=pltpu.SMEM)
    anyspace = pl.BlockSpec(memory_space=pltpu.HBM)
    bf16, f32 = jnp.bfloat16, jnp.float32
    dma = pltpu.SemaphoreType.DMA
    new_latent, decoded = pl.pallas_call(
        lambda *refs: attend_kernel(n, window, requests, *refs),
        name="attend",
        out_shape=(
            jax.ShapeDtypeStruct((patch, F_TOK), f32),
            jax.ShapeDtypeStruct((frames, 2 * rows, LCOLS, out_half), bf16),
        ),
        in_specs=[
            anyspace,
            anyspace,
            anyspace,
            anyspace,
            anyspace,
            anyspace,
            anyspace,
            anyspace,
            smem,
            smem,
            anyspace,
            anyspace,
            anyspace,
            anyspace,
        ],
        out_specs=(vmem,) * 2,
        scratch_shapes=[
            pltpu.VMEM((frames, (rows + 2) * PCOLS, patch), bf16),
            pltpu.VMEM((4, 12 * patch, 2 * ccols), bf16),
            pltpu.VMEM((1, 2 * ccols), f32),
            pltpu.VMEM((2 * up_rows, out_half), bf16),
            pltpu.VMEM((1, out_half), f32),
            pltpu.VMEM((2, frames * (rows + 2) * PCOLS, 2 * patch), bf16),
            pltpu.VMEM((4, frames * rows * PCOLS, 12 * patch), bf16),
            pltpu.VMEM((out_half // 128, frames, 2 * rows, LCOLS, 128), f32),
            pltpu.VMEM((3, F_TOK, 2 * half), bf16),
            pltpu.VMEM((taps, 2 * ccols), bf16),
            pltpu.VMEM((1, width), f32),
            pltpu.VMEM((1, width), f32),
            pltpu.VMEM((patch, width), bf16),
            pltpu.VMEM((patch, F_TOK), f32),
            pltpu.SMEM((1,), f32),
            pltpu.VMEM((2, F_TOK, half), bf16),
            pltpu.VMEM((slots, 2, F_TOK, half), bf16),
            pltpu.VMEM((half, width), bf16),
            pltpu.VMEM((F_TOK, width), bf16),
            pltpu.VMEM((2 * F_TOK, 2 * F_TOK), f32),
            pltpu.VMEM((heads, 2 * F_TOK, HD), f32),
            pltpu.VMEM((heads, 2 * F_TOK, HD), f32),
            pltpu.VMEM((heads, 2 * F_TOK, HD), f32),
            pltpu.VMEM((2 * F_TOK, half), bf16),
            pltpu.VMEM((chunks, F_TOK, chunk), bf16),
            pltpu.VMEM((chunks, F_TOK, chunk), bf16),
            pltpu.VMEM((F_TOK, width), f32),
            pltpu.VMEM((F_TOK, patch), bf16),
            dma((14,)),
            dma((2,)),
            dma((5 + 4 * hops,)),
            dma((slots,)),
            dma((chunks,)),
            dma((chunks,)),
            dma((3,)),
            dma((3,)),
            dma((2 * n - 1,)),
            dma((2 * n - 1,)),
        ],
        compiler_params=pltpu.CompilerParams(
            collective_id=0, has_side_effects=True, vmem_limit_bytes=67043328
        ),
    )(
        qkv[0].transpose(1, 0, 2),
        stream[0],
        out_weight,
        mod_scale,
        mod_shift,
        final_weight.T,
        latent[0].T,
        step_size,
        frame_counts,
        finished,
        conv_weight.reshape(taps, ccols),
        conv_bias[None],
        up_weight,
        up_bias[None],
    )
    return (new_latent.T[None], decoded[None])


def solution(mesh):
    fast = LROWS // mesh.shape["seq"] % 2 == 0 and mesh.shape["tp"] == 2
    in_specs = (
        P(("groups", "section"), ("seq", "tp"), None, None),
        P(("groups", "section"), ("seq", "tp"), None),
        P("tp", None),
        P(("groups", "section"), None),
        P(("groups", "section"), None),
        P(),
        P(("groups", "section"), ("seq", "tp"), None),
        P(("groups", "section")),
        P(("groups", "section"), None),
        P(("groups", "section"), None),
        P(None, None, None, None, "tp"),
        P("tp"),
        P("tp", None),
        P("tp"),
    )
    out_specs = (
        P(("groups", "section"), ("seq", "tp"), None),
        P(("groups", "section"), None, "seq", None, "tp"),
    )
    return jax.shard_map(
        on_device_fast if fast else on_device, mesh=mesh, in_specs=in_specs, out_specs=out_specs, check_vma=False
    )
```

profile of v0, /device:TPU:0, one launch (start us, length us, event | category | flops | bytes accessed | tf_op | source)
XLA Modules:
  0.0 59.4 jit_solution(13123413100520683681)
XLA Ops:
  1.3 54.8 %attend.1 = (f32[64,128]{1,0:T(8,128)}, bf16[8,4,32,256]{3,2,1,0:T(8,128)(2,1)}) custom-call(bf16[3,128,2048]{2,1,0:T(8,128)(2,1)} %bitcast.15, bf16[128,3072]{1,0:T(8,128)(2,1)} %bitcast.16, bf16[1024,3072]{1,0:T(8,128)(2,1)} %refs_2_.1, f32[1,3072]{1,0:T(1,128)} %refs_3_.1, f32[1,3072]{1,0:T(1,128)} %refs_4_.1, bf16[64,3072]{1,0:T(8,128)(2,1)} %bitcast.18, ...), custom_call_target="tpu_custom_call" | custom-call | tf_op jit(solution)/shard_map/attend/pallas_call | solution.py:809
  56.1 1.4 %copy.19 = f32[1,128,64]{1,2,0:T(8,128)} copy(f32[1,128,64]{1,2,0:T(8,128)} %bitcast.21) | data formatting | bytes 65536
  57.5 1.9 %copy.20 = bf16[1,8,4,32,256]{4,3,2,1,0:T(8,128)(2,1)} copy(bf16[1,8,4,32,256]{4,3,2,1,0:T(8,128)(2,1)} %bitcast.17) | data formatting | bytes 1048576
where the time goes:
time: 59.6 us; the launch traced here: 59.4 us
  Pallas kernels  54.8 us (92%)
  local copies, waits for them, and re-layouts  3.24 us (5%)
  between operations  1.29 us (2%)
    pallas_call x1, Pallas kernels, on_device_fast(): pl.pallas_call(lambda *refs: attend_kernel(n, window, requests, *refs), n...  54.8 us
    unnamed x2, local copies, waits for them, and re-layouts  3.24 us

commit v1 on v0

--- a/solution.py
+++ b/solution.py
@@ -265,8 +265,8 @@
     fw_hbm,
     latent_hbm,
     step_hbm,
-    counts_ref,
-    finished_ref,
+    counts_hbm,
+    finished_hbm,
     cw_ref,
     cb_ref,
     uw_ref,
@@ -288,6 +288,8 @@
     fw_ref,
     latent_ref,
     step_ref,
+    counts_ref,
+    finished_ref,
     q_buf,
     kv_buf,
     w_buf,
@@ -350,7 +352,11 @@
     get_w = pltpu.make_async_copy(ow_ref, w_buf, local_sems.at[2])
     get_stream = pltpu.make_async_copy(stream_ref, stream_buf, local_sems.at[3])
     stage = pltpu.make_async_copy(qkv_ref, qkv_buf, local_sems.at[13])
+    get_counts = pltpu.make_async_copy(counts_hbm, counts_ref, local_sems.at[14])
+    get_finished = pltpu.make_async_copy(finished_hbm, finished_ref, local_sems.at[15])
     stage.start()
+    get_counts.start()
+    get_finished.start()
     own_q.start()
     own_kv.start()
 
@@ -361,6 +367,8 @@
         )
     pl.semaphore_wait(barrier, devices - 1)
     stage.wait()
+    get_counts.wait()
+    get_finished.wait()
 
     def kv_copy(target_tp, target_seq, slot, send):
         return remote(
@@ -616,7 +624,7 @@
         velocity = velocity + lax.dot_general(
             fw_ref[:, span], modulated, NT, preferred_element_type=jnp.float32
         )
-    updated = latent_ref[...] + step_ref[0] * velocity
+    updated = latent_ref[...] + step_ref[0, 0] * velocity
     new_latent_ref[...] = updated
     own_video[...] = updated.T.astype(jnp.bfloat16)
     kept = video_ref.shape[1]
@@ -802,7 +810,6 @@
     chunks = 6
     chunk = width // chunks
     vmem = pl.BlockSpec(memory_space=pltpu.VMEM)
-    smem = pl.BlockSpec(memory_space=pltpu.SMEM)
     anyspace = pl.BlockSpec(memory_space=pltpu.HBM)
     bf16, f32 = jnp.bfloat16, jnp.float32
     dma = pltpu.SemaphoreType.DMA
@@ -822,8 +829,8 @@
             anyspace,
             anyspace,
             anyspace,
-            smem,
-            smem,
+            anyspace,
+            anyspace,
             anyspace,
             anyspace,
             anyspace,
@@ -845,7 +852,9 @@
             pltpu.VMEM((1, width), f32),
             pltpu.VMEM((patch, width), bf16),
             pltpu.VMEM((patch, F_TOK), f32),
-            pltpu.SMEM((1,), f32),
+            pltpu.SMEM((1, 1), f32),
+            pltpu.SMEM((1, requests), jnp.int32),
+            pltpu.SMEM((1, requests), jnp.int32),
             pltpu.VMEM((2, F_TOK, half), bf16),
             pltpu.VMEM((slots, 2, F_TOK, half), bf16),
             pltpu.VMEM((half, width), bf16),
@@ -859,7 +868,7 @@
             pltpu.VMEM((chunks, F_TOK, chunk), bf16),
             pltpu.VMEM((F_TOK, width), f32),
             pltpu.VMEM((F_TOK, patch), bf16),
-            dma((14,)),
+            dma((16,)),
             dma((2,)),
             dma((5 + 4 * hops,)),
             dma((slots,)),
@@ -871,23 +880,28 @@
             dma((2 * n - 1,)),
         ],
         compiler_params=pltpu.CompilerParams(
-            collective_id=0, has_side_effects=True, vmem_limit_bytes=67043328
+            collective_id=0, has_side_effects=True, vmem_limit_bytes=41943040
         ),
     )(
-        qkv[0].transpose(1, 0, 2),
-        stream[0],
-        out_weight,
-        mod_scale,
-        mod_shift,
-        final_weight.T,
-        latent[0].T,
-        step_size,
-        frame_counts,
-        finished,
-        conv_weight.reshape(taps, ccols),
-        conv_bias[None],
-        up_weight,
-        up_bias[None],
+        *(
+            value if value.size == 1 else pltpu.with_memory_space_constraint(value, pltpu.HBM)
+            for value in (
+                qkv[0].transpose(1, 0, 2),
+                stream[0],
+                out_weight,
+                mod_scale,
+                mod_shift,
+                final_weight.T,
+                latent[0].T,
+                step_size[None],
+                frame_counts,
+                finished,
+                conv_weight.reshape(taps, ccols),
+                conv_bias[None],
+                up_weight,
+                up_bias[None],
+            )
+        )
     )
     return (new_latent.T[None], decoded[None])
 

time: 59.6 us -> 56.3 us (0.945)
  local copies, waits for them, and re-layouts: 3.24 us -> 1.41 us
  Pallas kernels: 54.8 us -> 53.4 us
    unnamed x2, local copies, waits for them, and re-layouts: 3.24 us -> 1.41 us
    pallas_call x1, Pallas kernels: 54.8 us -> 53.4 us  [on_device_fast(): pl.pallas_call(lambda *refs: attend_kernel(n, window, requests, *refs), n...]
where the time goes in v1:
time: 56.3 us; the launch traced here: 56.1 us
  Pallas kernels  53.4 us (95%)
  local copies, waits for them, and re-layouts  1.41 us (3%)
  between operations  1.29 us (2%)
    pallas_call x1, Pallas kernels, on_device_fast(): pl.pallas_call(lambda *refs: attend_kernel(n, window, requests, *refs), n...  53.4 us
    unnamed x2, local copies, waits for them, and re-layouts  1.41 us

profile of v1, /device:TPU:0, one launch (start us, length us, event | category | flops | bytes accessed | tf_op | source)
XLA Modules:
  0.0 56.1 jit_solution(9755430908345565137)
XLA Ops:
  1.3 53.4 %attend.1 = (f32[64,128]{1,0:T(8,128)S(1)}, bf16[8,4,32,256]{3,2,1,0:T(8,128)(2,1)S(1)}) custom-call(bf16[3,128,2048]{2,1,0:T(8,128)(2,1)} %bitcast.19, bf16[128,3072]{1,0:T(8,128)(2,1)} %bitcast.20, bf16[1024,3072]{1,0:T(8,128)(2,1)} %refs_2_.1, f32[1,3072]{1,0:T(1,128)} %refs_3_.1, f32[1,3072]{1,0:T(1,128)} %refs_4_.1, bf16[64,3072]{1,0:T(8,128)(2,1)} %bitcast.21, ...), custom_call_target="tpu_custom_call" | custom-call | tf_op jit(solution)/shard_map/attend/pallas_call | solution.py:816
  54.7 0.6 %copy.19 = f32[1,128,64]{1,2,0:T(8,128)} copy(f32[1,128,64]{1,2,0:T(8,128)S(1)} %bitcast.18) | data formatting | bytes 65536
  55.3 0.8 %copy.20 = bf16[1,8,4,32,256]{4,3,2,1,0:T(8,128)(2,1)} copy(bf16[1,8,4,32,256]{4,3,2,1,0:T(8,128)(2,1)S(1)} %bitcast.17) | data formatting | bytes 1048576

commit v2 on v1

--- a/solution.py
+++ b/solution.py
@@ -255,7 +255,6 @@
 
 def attend_kernel(
     n,
-    window,
     requests,
     qkv_ref,
     stream_ref,
@@ -281,7 +280,6 @@
     shifted,
     columns,
     spread,
-    qkv_buf,
     cw2_ref,
     scale_ref,
     shift_ref,
@@ -290,23 +288,24 @@
     step_ref,
     counts_ref,
     finished_ref,
-    q_buf,
-    kv_buf,
+    units,
+    give,
+    outgoing,
+    incoming,
     w_buf,
     stream_buf,
     bias_buf,
-    max_buf,
-    sum_buf,
+    att_buf,
     acc_buf,
-    att_buf,
     part_buf,
     got_buf,
     mixed_buf,
     own_video,
     local_sems,
-    q_sems,
-    kv_send,
-    kv_recv,
+    swap_send,
+    swap_recv,
+    unit_send,
+    unit_recv,
     part_send,
     part_recv,
     wt_send,
@@ -319,11 +318,12 @@
     o = 1 - t
     me = s * 2 + t
     devices = 2 * n
-    half = q_buf.shape[2]
-    heads = half // HD
-    hops = (window + 1) // 2
+    groups = units.shape[0]
+    lanes = units.shape[4]
     out_half = uw_ref.shape[1] // 2
     ccols = cw_ref.shape[1]
+    has_left = s > 0
+    has_right = s < n - 1
 
     def at(seq, tp):
         return {"seq": seq, "tp": tp}
@@ -345,20 +345,28 @@
     def cols(which, width):
         return pl.ds(pl.multiple_of(which * width, width), width)
 
-    own_q = pltpu.make_async_copy(qkv_ref.at[0, :, cols(t, half)], q_buf.at[1], local_sems.at[0])
-    own_kv = pltpu.make_async_copy(
-        qkv_ref.at[1:3, :, cols(t, half)], kv_buf.at[window + t], local_sems.at[1]
-    )
+    get_counts = pltpu.make_async_copy(counts_hbm, counts_ref, local_sems.at[0])
+    get_finished = pltpu.make_async_copy(finished_hbm, finished_ref, local_sems.at[1])
     get_w = pltpu.make_async_copy(ow_ref, w_buf, local_sems.at[2])
     get_stream = pltpu.make_async_copy(stream_ref, stream_buf, local_sems.at[3])
-    stage = pltpu.make_async_copy(qkv_ref, qkv_buf, local_sems.at[13])
-    get_counts = pltpu.make_async_copy(counts_hbm, counts_ref, local_sems.at[14])
-    get_finished = pltpu.make_async_copy(finished_hbm, finished_ref, local_sems.at[15])
-    stage.start()
+    theirs = [
+        pltpu.make_async_copy(
+            qkv_ref.at[:, :, cols(o * groups + c, lanes)], give.at[c], local_sems.at[13 + c]
+        )
+        for c in range(groups)
+    ]
+    own = [
+        pltpu.make_async_copy(
+            qkv_ref.at[:, :, cols(t * groups + c, lanes)], units.at[c, t], local_sems.at[13 + groups + c]
+        )
+        for c in range(groups)
+    ]
+    for c in range(groups):
+        theirs[c].start()
+    for c in range(groups):
+        own[c].start()
     get_counts.start()
     get_finished.start()
-    own_q.start()
-    own_kv.start()
 
     barrier = pltpu.get_barrier_semaphore()
     for k in range(1, devices):
@@ -366,40 +374,90 @@
             barrier, inc=1, device_id=peer_of(k), device_id_type=pl.DeviceIdType.MESH
         )
     pl.semaphore_wait(barrier, devices - 1)
-    stage.wait()
+
+    swaps = [
+        remote(give.at[c], units.at[c, t], swap_send.at[c], swap_recv.at[c], at(s, o))
+        for c in range(groups)
+    ]
+    for c in range(groups):
+        theirs[c].wait()
+        swaps[c].start()
+
     get_counts.wait()
     get_finished.wait()
-
-    def kv_copy(target_tp, target_seq, slot, send):
-        return remote(
-            qkv_buf.at[1:3, :, cols(target_tp, half)],
-            kv_buf.at[slot],
-            kv_send.at[send],
-            kv_recv.at[slot],
-            at(target_seq, target_tp),
-        )
-
-    has_left = s > 0
-    has_right = s < n - 1
-    rights = [kv_copy(k, s + 1, window + t - 2, k) for k in range(2)]
-    lefts = [kv_copy(k, s - 1, window + t + 2, 2 + k) for k in range(2)]
-    partner_q = remote(
-        qkv_buf.at[0, :, cols(o, half)], q_buf.at[0], q_sems.at[0], q_sems.at[1], at(s, o)
-    )
-    partner_kv = kv_copy(o, s, window + t, 4)
-
-    @pl.when(has_right)
-    def _():
-        for copy in rights:
-            copy.start()
-
-    @pl.when(has_left)
-    def _():
-        for copy in lefts:
-            copy.start()
-
-    partner_q.start()
-    partner_kv.start()
+    ends = frame_ends(counts_ref, requests)
+
+    def request(frame):
+        return jnp.where(frame < 0, -1, request_of(frame, ends))
+
+    req = {k: request(s * 2 + k) for k in range(-2, 4)}
+    left_tied = req[-1] == req[0]
+    right_tied = req[1] == req[2]
+    left_two = req[-2] == req[-1]
+    own_two = req[0] == req[1]
+    right_two = req[2] == req[3]
+    pair_left = jnp.logical_and(left_tied, jnp.logical_and(left_two, own_two))
+    pair_right = jnp.logical_and(right_tied, jnp.logical_and(own_two, right_two))
+    paired = jnp.logical_or(pair_left, pair_right)
+    away_left = jnp.logical_and(left_tied, jnp.logical_and(left_two, jnp.logical_not(own_two)))
+    away_right = jnp.logical_and(right_tied, jnp.logical_not(own_two))
+    pairs = (pair_left, pair_right)
+
+    def pair_unit(u):
+        place = u % 4
+        return units[u // 4, place % 2, 1 + place // 2]
+
+    def guest_unit(side, u):
+        return units[u // 3, side, u % 3]
+
+    guest_units = 3 * groups
+    sends = [[], []]
+    for u in range(4 * groups):
+        for side, step in ((0, -1), (1, 1)):
+            sends[side].append(
+                remote(
+                    outgoing.at[side, u],
+                    incoming.at[1 - side, u],
+                    unit_send.at[side, u],
+                    unit_recv.at[1 - side, u],
+                    at(s + step, t),
+                )
+            )
+
+    def start(first, count):
+        @pl.when(has_right)
+        def _():
+            for u in range(first, first + count):
+                sends[1][u].start()
+
+        @pl.when(has_left)
+        def _():
+            for u in range(first, first + count):
+                sends[0][u].start()
+
+    def arrived(first, count):
+        @pl.when(has_left)
+        def _():
+            for u in range(first, first + count):
+                remote(
+                    incoming.at[0, u], incoming.at[0, u], unit_send.at[0, u], unit_recv.at[0, u], at(s, o)
+                ).wait_recv()
+
+        @pl.when(has_right)
+        def _():
+            for u in range(first, first + count):
+                remote(
+                    incoming.at[1, u], incoming.at[1, u], unit_send.at[1, u], unit_recv.at[1, u], at(s, o)
+                ).wait_recv()
+
+    for c in range(groups):
+        own[c].wait()
+        swaps[c].wait_recv()
+        for u in range(3 * c, 3 * c + 3):
+            for side in range(2):
+                outgoing[side, u] = lax.select(pairs[side], pair_unit(u), guest_unit(side, u))
+        start(3 * c, 3)
+
     give_cw = remote(cw_ref, cw2_ref.at[:, ccols:], wt_send.at[0], wt_recv.at[0], at(s, o))
     give_cb = remote(cb_ref, cb2_ref.at[:, ccols:], wt_send.at[1], wt_recv.at[1], at(s, o))
     give_uw = remote(
@@ -433,175 +491,165 @@
     get_stream.start()
     get_w.start()
 
-    ends = frame_ends(counts_ref, requests)
-    query_req = (request_of(s * 2 + o, ends), request_of(s * 2 + t, ends))
-    score_scale = 1.0 / math.sqrt(HD)
-
-    def wait_slot(slot):
-        remote(kv_buf.at[slot], kv_buf.at[slot], kv_send.at[0], kv_recv.at[slot], at(s, o)).wait_recv()
-
-    def attend_far(slot, place, query_frame):
-        key_req = request_of(s * 2 - window + slot, ends)
-        bias = jnp.where(request_of(query_frame, ends) == key_req, 0.0, NEG_FILL).astype(jnp.float32)
-        rows = pl.ds(pl.multiple_of(place * F_TOK, F_TOK), F_TOK)
-
-        def one_head(h, carry):
-            lanes = pl.ds(pl.multiple_of(h * HD, HD), HD)
-            q = q_buf[place, :, lanes]
-            scores = lax.dot_general(
-                q, kv_buf[slot, 0, :, lanes], NT, preferred_element_type=jnp.float32
-            )
-            scores = scores * score_scale + bias
-            old = max_buf[h, rows, :]
-            top = jnp.maximum(old, jnp.max(scores, axis=1, keepdims=True))
-            weights = jnp.exp(scores - top)
-            factor = jnp.exp(old - top)
-            sum_buf[h, rows, :] = sum_buf[h, rows, :] * factor + jnp.sum(
-                weights, axis=1, keepdims=True
-            )
-            acc_buf[h, rows, :] = acc_buf[h, rows, :] * factor + lax.dot_general(
-                weights.astype(jnp.bfloat16),
-                kv_buf[slot, 1, :, lanes],
-                NN,
-                preferred_element_type=jnp.float32,
-            )
-            return carry
-
-        lax.fori_loop(0, heads, one_head, 0, unroll=True)
-
-    def attend(first, width, fresh):
-        for i in range(2):
-            for j in range(width):
-                key_req = request_of(s * 2 - window + first + j, ends)
-                bias = jnp.where(query_req[i] == key_req, 0.0, NEG_FILL).astype(jnp.float32)
-                bias_buf[pl.ds(i * F_TOK, F_TOK), pl.ds(j * F_TOK, F_TOK)] = jnp.full(
+    @pl.when(jnp.logical_not(has_left))
+    def _():
+        incoming[0] = jnp.zeros(incoming.shape[1:], incoming.dtype)
+
+    @pl.when(jnp.logical_not(has_right))
+    def _():
+        incoming[1] = jnp.zeros(incoming.shape[1:], incoming.dtype)
+
+    def fill_bias(which, rows, keys, open_ends):
+        for i, row in enumerate(rows):
+            for j, key in enumerate(keys):
+                allowed = req[row] == req[key]
+                if open_ends and j in (0, 3):
+                    allowed = jnp.logical_or(paired, allowed)
+                bias = jnp.where(allowed, 0.0, NEG_FILL).astype(jnp.float32)
+                bias_buf[which, pl.ds(i * F_TOK, F_TOK), pl.ds(j * F_TOK, F_TOK)] = jnp.full(
                     (F_TOK, F_TOK), bias, jnp.float32
                 )
-        bias = bias_buf[:, : width * F_TOK]
-
-        def one_head(h, carry):
-            lanes = pl.ds(pl.multiple_of(h * HD, HD), HD)
-            q = q_buf[:, :, lanes].reshape(2 * F_TOK, HD)
-            keys = kv_buf[first : first + width, 0, :, lanes].reshape(width * F_TOK, HD)
-            values = kv_buf[first : first + width, 1, :, lanes].reshape(width * F_TOK, HD)
-            scores = lax.dot_general(q, keys, NT, preferred_element_type=jnp.float32)
-            scores = scores * score_scale + bias
-            top = jnp.max(scores, axis=1, keepdims=True)
-            if not fresh:
-                old = max_buf[h]
-                top = jnp.maximum(old[:, :1], top)
-            weights = jnp.exp(scores - top)
-            total = jnp.sum(weights, axis=1, keepdims=True)
-            product = lax.dot_general(
-                weights.astype(jnp.bfloat16), values, NN, preferred_element_type=jnp.float32
-            )
-            if not fresh:
-                factor = jnp.exp(old[:, :1] - top)
-                total = total + sum_buf[h][:, :1] * factor
-                product = product + acc_buf[h] * factor
-            max_buf[h] = jnp.broadcast_to(top, (2 * F_TOK, HD))
-            sum_buf[h] = jnp.broadcast_to(total, (2 * F_TOK, HD))
-            acc_buf[h] = product
-            return carry
-
-        lax.fori_loop(0, heads, one_head, 0, unroll=4)
-
-    own_q.wait()
-    own_kv.wait()
-    partner_q.wait_recv()
-    wait_slot(window + o)
-    attend(window, 2, True)
+
+    fill_bias(0, (0, 1), (-1, 0, 1, 2), True)
+    fill_bias(1, (-1, 2), (-1, 0, 1, 2), False)
+    score_scale = 1.0 / math.sqrt(HD)
+
+    def weigh(queries, keys, which):
+        scores = lax.dot_general(queries, keys, NT, preferred_element_type=jnp.float32)
+        scores = scores * score_scale + bias_buf[which]
+        weights = jnp.exp(scores - jnp.max(scores, axis=1, keepdims=True))
+        return weights.astype(jnp.bfloat16), jnp.sum(weights, axis=1, keepdims=True)
+
+    def gather(weights, total, values):
+        product = lax.dot_general(weights, values, NN, preferred_element_type=jnp.float32)
+        return (product / total).astype(jnp.bfloat16)
+
+    def head(h):
+        return pl.ds(h * HD, HD)
+
+    heads = range(lanes // HD)
+
+    def attend_guests(c):
+        for h in heads:
+            span = head(h)
+
+            def joined(which):
+                return jnp.concatenate(
+                    [
+                        incoming[0, 3 * c + which, :, span],
+                        units[c, 0, which, :, span],
+                        units[c, 1, which, :, span],
+                        incoming[1, 3 * c + which, :, span],
+                    ],
+                    axis=0,
+                )
+
+            queries = jnp.concatenate([incoming[0, 3 * c, :, span], incoming[1, 3 * c, :, span]], axis=0)
+            weights, total = weigh(queries, joined(1), 1)
+            result = gather(weights, total, joined(2))
+            u = guest_units + c
+            place = u % 4
+            pair = units[u // 4, place % 2, 1 + place // 2, :, span]
+            for side in range(2):
+                outgoing[side, u, :, span] = lax.select(
+                    pairs[side], pair, result[side * F_TOK : (side + 1) * F_TOK]
+                )
+        start(guest_units + c, 1)
+
+    def far(c, which, end, span):
+        u = 4 * c + 2 * (which - 1) + end
+        other = incoming[end, 3 * c + which, :, span]
+        other = lax.select(pair_right, incoming[1, u, :, span], other)
+        return lax.select(pair_left, incoming[0, u, :, span], other)
+
+    def joined_own(c, which, span):
+        return jnp.concatenate(
+            [
+                far(c, which, 0, span),
+                units[c, 0, which, :, span],
+                units[c, 1, which, :, span],
+                far(c, which, 1, span),
+            ],
+            axis=0,
+        )
+
+    def weigh_own(c):
+        found = []
+        for h in heads:
+            queries = jnp.concatenate([units[c, 0, 0, :, head(h)], units[c, 1, 0, :, head(h)]], axis=0)
+            found.append(weigh(queries, joined_own(c, 1, head(h)), 0))
+        return found
+
+    def gather_own(c, found):
+        for h in heads:
+            weights, total = found[h]
+            att_buf[c, :, head(h)] = gather(weights, total, joined_own(c, 2, head(h)))
+
+    def attended(c):
+        u = guest_units + c
+        return jnp.concatenate(
+            [
+                lax.select(away_left, incoming[0, u], att_buf[c, :F_TOK]),
+                lax.select(away_right, incoming[1, u], att_buf[c, F_TOK:]),
+            ],
+            axis=0,
+        )
+
+    chunks, _, chunk = part_buf.shape
+
+    def project(first, count):
+        ready = jnp.concatenate([attended(c) for c in range(first, first + count)], axis=1)
+        rows = pl.ds(first * lanes, count * lanes)
+        for j in range(chunks):
+            span = pl.ds(j * chunk, chunk)
+            result = lax.dot_general(ready, w_buf[rows, span], NN, preferred_element_type=jnp.float32)
+            acc_buf[:, span] = result if first == 0 else acc_buf[:, span] + result
 
     loads[0].wait()
     give_cw.wait()
     expanded_ref[...] = jnp.zeros_like(expanded_ref)
     expand_weight(cw2_ref, expanded_ref, new_latent_ref.shape[0])
 
-    relays = []
-    for d in range(1, hops + 1):
-        low = window - 2 * d
-        high = window + 2 * d
-        two = 2 * d <= window
-        more = d < hops
-
-        def receive(first, width, good, forward, good_next, step, base, sends):
-            @pl.when(good)
-            def _():
-                for j in range(width):
-                    wait_slot(first + j)
-
-            copies = []
-            if forward:
-                for slot in forward:
-                    copies.append(
-                        remote(
-                            kv_buf.at[slot],
-                            kv_buf.at[slot - 2 * step],
-                            kv_send.at[sends + len(copies)],
-                            kv_recv.at[slot - 2 * step],
-                            at(s + step, t),
-                        )
-                    )
-
-                @pl.when(good_next)
-                def _():
-                    for copy in copies:
-                        copy.start()
-
-            return [(copy, good_next) for copy in copies]
-
-        base = 5 + 4 * (d - 1)
-        wide = 2 if two else 1
-        next_two = 2 * (d + 1) <= window
-        left_first = low if two else low + 1
-        left_good = s >= d
-        right_good = s <= n - 1 - d
-        left_fwd = ([low, low + 1] if next_two else [low + 1]) if more else []
-        right_fwd = ([high, high + 1] if next_two else [high]) if more else []
-        def attend_left():
-            @pl.when(left_good)
-            def _():
-                if two:
-                    attend(left_first, 2, False)
-                else:
-                    attend_far(left_first, o, s * 2)
-
-        relays += receive(
-            left_first, wide, left_good, left_fwd, jnp.logical_and(left_good, has_right), 1, d, base
-        )
-        if not more:
-            attend_left()
-        relays += receive(
-            high, wide, right_good, right_fwd, jnp.logical_and(right_good, has_left), -1, d, base + 2
-        )
-        if more:
-            attend_left()
-
-        @pl.when(right_good)
-        def _():
-            if two:
-                attend(high, 2, False)
-            else:
-                attend_far(high, t, s * 2 + 1)
-
-    for h in range(heads):
-        att_buf[:, h * HD : (h + 1) * HD] = (acc_buf[h] / sum_buf[h]).astype(jnp.bfloat16)
-
+    arrived(0, 3)
+    attend_guests(0)
+    arrived(3, 1)
+    gather_own(0, weigh_own(0))
+    arrived(4, 2)
+    attend_guests(1)
+    arrived(6, 2)
+    gather_own(1, weigh_own(1))
+    arrived(8, 1)
+    attend_guests(2)
+    arrived(9, 3)
+    attend_guests(3)
+    gather_own(2, weigh_own(2))
     get_w.wait()
     get_stream.wait()
     for load in loads[1:]:
         load.wait()
-    chunks, _, chunk = part_buf.shape
-    attended = att_buf[...]
+    arrived(12, 2)
+    project(0, 2)
+    found = weigh_own(3)
+    arrived(14, 1)
+    project(2, 1)
+    arrived(15, 1)
+    gather_own(3, found)
+
+    ready = attended(3)
     parts = []
     for c in range(chunks):
         span = pl.ds(c * chunk, chunk)
-        result = lax.dot_general(attended, w_buf[:, span], NN, preferred_element_type=jnp.float32)
-        part_buf[c] = result[:F_TOK].astype(jnp.bfloat16)
+        result = acc_buf[:, span] + lax.dot_general(
+            ready, w_buf[pl.ds(3 * lanes, lanes), span], NN, preferred_element_type=jnp.float32
+        )
+        first_rows, second_rows = result[:F_TOK], result[F_TOK:]
+        part_buf[c] = lax.select(t == 0, second_rows, first_rows).astype(jnp.bfloat16)
         copy = remote(part_buf.at[c], got_buf.at[c], part_send.at[c], part_recv.at[c], at(s, o))
         copy.start()
         parts.append(copy)
-        mixed_buf[:, span] = result[F_TOK:] + stream_buf[:, span].astype(jnp.float32)
+        mixed_buf[:, span] = lax.select(t == 0, first_rows, second_rows) + stream_buf[:, span].astype(
+            jnp.float32
+        )
     row_sum = jnp.zeros((F_TOK, 1), jnp.float32)
     for c in range(chunks):
         span = pl.ds(c * chunk, chunk)
@@ -633,7 +681,7 @@
         first = slab_start(seq, kept // PCOLS - 2) * PCOLS
         return pl.ds(pl.multiple_of(first, PCOLS), kept)
 
-    sends = []
+    videos = []
     for k in range(1, devices):
         target = peer_of(k)
         copy = remote(
@@ -644,33 +692,27 @@
             target,
         )
         copy.start()
-        sends.append(copy)
+        videos.append(copy)
     video_ref[me] = own_video[needed(s), :]
 
-    partner_q.wait_send()
-    partner_kv.wait_send()
+    for copy in swaps:
+        copy.wait_send()
 
     @pl.when(has_right)
     def _():
-        for copy in rights:
+        for copy in sends[1]:
             copy.wait_send()
 
     @pl.when(has_left)
     def _():
-        for copy in lefts:
-            copy.wait_send()
-
-    for copy, good in relays:
-
-        @pl.when(good)
-        def _(copy=copy):
+        for copy in sends[0]:
             copy.wait_send()
 
     for copy in parts:
         copy.wait_send()
     give_cb.wait()
     give_uw.wait()
-    for copy in sends:
+    for copy in videos:
         copy.wait()
     decode_frames(
         kept // PCOLS - 2,
@@ -794,18 +836,16 @@
 ):
     n = lax.axis_size("seq")
     frames = 2 * n
-    window = frames // 2 - 1
     requests = frame_counts.shape[1]
     width = stream.shape[2]
     patch = latent.shape[2]
     half = out_weight.shape[0]
-    heads = half // HD
     ccols = conv_weight.shape[4]
     taps = conv_weight.shape[0] * conv_weight.shape[1] * conv_weight.shape[2] * LATC
     up_rows, up_all = up_weight.shape
     out_half = up_all // 2
-    slots = 2 * window + 2
-    hops = (window + 1) // 2
+    groups = 4
+    lanes = half // groups
     rows = PROWS // n
     chunks = 6
     chunk = width // chunks
@@ -814,7 +854,7 @@
     bf16, f32 = jnp.bfloat16, jnp.float32
     dma = pltpu.SemaphoreType.DMA
     new_latent, decoded = pl.pallas_call(
-        lambda *refs: attend_kernel(n, window, requests, *refs),
+        lambda *refs: attend_kernel(n, requests, *refs),
         name="attend",
         out_shape=(
             jax.ShapeDtypeStruct((patch, F_TOK), f32),
@@ -846,7 +886,6 @@
             pltpu.VMEM((2, frames * (rows + 2) * PCOLS, 2 * patch), bf16),
             pltpu.VMEM((4, frames * rows * PCOLS, 12 * patch), bf16),
             pltpu.VMEM((out_half // 128, frames, 2 * rows, LCOLS, 128), f32),
-            pltpu.VMEM((3, F_TOK, 2 * half), bf16),
             pltpu.VMEM((taps, 2 * ccols), bf16),
             pltpu.VMEM((1, width), f32),
             pltpu.VMEM((1, width), f32),
@@ -855,23 +894,24 @@
             pltpu.SMEM((1, 1), f32),
             pltpu.SMEM((1, requests), jnp.int32),
             pltpu.SMEM((1, requests), jnp.int32),
-            pltpu.VMEM((2, F_TOK, half), bf16),
-            pltpu.VMEM((slots, 2, F_TOK, half), bf16),
+            pltpu.VMEM((groups, 2, 3, F_TOK, lanes), bf16),
+            pltpu.VMEM((groups, 3, F_TOK, lanes), bf16),
+            pltpu.VMEM((2, 4 * groups, F_TOK, lanes), bf16),
+            pltpu.VMEM((2, 4 * groups, F_TOK, lanes), bf16),
             pltpu.VMEM((half, width), bf16),
             pltpu.VMEM((F_TOK, width), bf16),
-            pltpu.VMEM((2 * F_TOK, 2 * F_TOK), f32),
-            pltpu.VMEM((heads, 2 * F_TOK, HD), f32),
-            pltpu.VMEM((heads, 2 * F_TOK, HD), f32),
-            pltpu.VMEM((heads, 2 * F_TOK, HD), f32),
-            pltpu.VMEM((2 * F_TOK, half), bf16),
+            pltpu.VMEM((2, 2 * F_TOK, 4 * F_TOK), f32),
+            pltpu.VMEM((groups, 2 * F_TOK, lanes), bf16),
+            pltpu.VMEM((2 * F_TOK, width), f32),
             pltpu.VMEM((chunks, F_TOK, chunk), bf16),
             pltpu.VMEM((chunks, F_TOK, chunk), bf16),
             pltpu.VMEM((F_TOK, width), f32),
             pltpu.VMEM((F_TOK, patch), bf16),
-            dma((16,)),
-            dma((2,)),
-            dma((5 + 4 * hops,)),
-            dma((slots,)),
+            dma((13 + 2 * groups,)),
+            dma((groups,)),
+            dma((groups,)),
+            dma((2, 4 * groups)),
+            dma((2, 4 * groups)),
             dma((chunks,)),
             dma((chunks,)),
             dma((3,)),
@@ -907,7 +947,7 @@
 
 
 def solution(mesh):
-    fast = LROWS // mesh.shape["seq"] % 2 == 0 and mesh.shape["tp"] == 2
+    fast = mesh.shape["seq"] == 4 and mesh.shape["tp"] == 2
     in_specs = (
         P(("groups", "section"), ("seq", "tp"), None, None),
         P(("groups", "section"), ("seq", "tp"), None),

time: 56.3 us -> 44.6 us (0.79)
  Pallas kernels: 53.4 us -> 41.8 us
    pallas_call x1, Pallas kernels: 53.4 us -> 41.8 us  [on_device_fast(): pl.pallas_call(lambda *refs: attend_kernel(n, requests, *refs), name='att...]
where the time goes in v2:
time: 44.6 us; the launch traced here: 44.5 us
  Pallas kernels  41.8 us (94%)
  local copies, waits for them, and re-layouts  1.41 us (3%)
  between operations  1.29 us (3%)
    pallas_call x1, Pallas kernels, on_device_fast(): pl.pallas_call(lambda *refs: attend_kernel(n, requests, *refs), name='att...  41.8 us
    unnamed x2, local copies, waits for them, and re-layouts  1.41 us

profile of v2, /device:TPU:0, one launch (start us, length us, event | category | flops | bytes accessed | tf_op | source)
XLA Modules:
  0.0 44.5 jit_solution(6600065133655436583)
XLA Ops:
  1.3 41.8 %attend.1 = (f32[64,128]{1,0:T(8,128)S(1)}, bf16[8,4,32,256]{3,2,1,0:T(8,128)(2,1)S(1)}) custom-call(bf16[3,128,2048]{2,1,0:T(8,128)(2,1)} %bitcast.19, bf16[128,3072]{1,0:T(8,128)(2,1)} %bitcast.20, bf16[1024,3072]{1,0:T(8,128)(2,1)} %refs_2_.1, f32[1,3072]{1,0:T(1,128)} %refs_3_.1, f32[1,3072]{1,0:T(1,128)} %refs_4_.1, bf16[64,3072]{1,0:T(8,128)(2,1)} %bitcast.21, ...), custom_call_target="tpu_custom_call" | custom-call | tf_op jit(solution)/shard_map/attend/pallas_call | solution.py:856
  43.1 0.6 %copy.19 = f32[1,128,64]{1,2,0:T(8,128)} copy(f32[1,128,64]{1,2,0:T(8,128)S(1)} %bitcast.18) | data formatting | bytes 65536
  43.7 0.8 %copy.20 = bf16[1,8,4,32,256]{4,3,2,1,0:T(8,128)(2,1)} copy(bf16[1,8,4,32,256]{4,3,2,1,0:T(8,128)(2,1)S(1)} %bitcast.17) | data formatting | bytes 1048576
